TPU v7x, 32 devices: a whole 2x2x4 slice. The times are simulated.
32 devices in a mesh: iface: 8 (over z, y), dom: 4 (over x, core).
Axes of the slice: x: 2, y: 2, z: 4, core: 2. Of those that a mesh axis runs over, the one named last changes fastest.
Arguments:
- interface: float32 [131072], P(('iface', 'dom')), may hold values from -6 to 6
- previous_residual: float32 [131072], P(('iface', 'dom')), may hold values from -6 to 6
- previous_estimate: float32 [131072], P(('iface', 'dom')), may hold values from -6 to 6
- forcing: float32 [131072], P(('iface', 'dom')), may hold values from -60 to 60
- stiffness: float32 [131072], P(('iface', 'dom')), may hold values from 0.2 to 0.6
- history_residual: float32 [100, 131072], P(None, ('iface', 'dom')), may hold values from -40 to 40
- history_estimate: float32 [100, 131072], P(None, ('iface', 'dom')), may hold values from -6 to 6
Outputs:
- interface_next: float32 [131072], P(('iface', 'dom'))
- residual_last: float32 [131072], P(('iface', 'dom'))
All inputs are finite; a program needn't handle non-finite values.
Results may differ from a plain program's by a relative error of at most 0.0003.
Values sent between devices are 32-bit elements; how exact they have to be, the bound alone decides.
A program may use at most 64 MiB of HBM per device.

v0:
```python
import jax
import jax.numpy as jnp
from jax import lax
from jax.sharding import PartitionSpec as P

ITERS = 3


coupling = 0.25


def from_behind(value, axis, steps):
    count = lax.axis_size(axis)
    initial, last = (max(0, -steps), min(count, count - steps))
    return lax.ppermute(value, axis, [(source, source + steps) for source in range(initial, last)])


def solver_map(current, forcing, stiffness):
    from_left = from_behind(current[-1:], ("iface", "dom"), 1)
    from_right = from_behind(current[:1], ("iface", "dom"), -1)
    padded = jnp.concatenate([from_left, current, from_right], axis=0)
    return forcing + stiffness * jnp.tanh(current) + coupling * (padded[:-2] + padded[2:])


def shards(
    interface,
    previous_residual,
    previous_estimate,
    forcing,
    stiffness,
    history_residual,
    history_estimate,
):
    high = lax.Precision.HIGHEST
    current = interface
    hist_v = history_residual
    hist_w = history_estimate
    old_residual = previous_residual
    old_estimate = previous_estimate
    residual = previous_residual
    for iteration in range(ITERS):
        estimate = solver_map(current, forcing, stiffness)
        residual = estimate - current
        new_column = residual - old_residual
        hist_v = jnp.concatenate([hist_v, new_column[None, :]], axis=0)
        hist_w = jnp.concatenate([hist_w, (estimate - old_estimate)[None, :]], axis=0)
        gram_matrix, projection = lax.psum(
            (jnp.dot(hist_v, hist_v.T, precision=high), jnp.dot(hist_v, residual, precision=high)),
            ("iface", "dom"),
        )
        factor = jnp.linalg.cholesky(gram_matrix)
        coeffs = -jax.scipy.linalg.cho_solve((factor, True), projection)
        current = estimate + jnp.dot(coeffs, hist_w, precision=high)
        old_residual = residual
        old_estimate = estimate
    return (current, residual)


def solution(mesh):
    return jax.shard_map(
        shards,
        mesh=mesh,
        in_specs=(
            P(("iface", "dom")),
            P(("iface", "dom")),
            P(("iface", "dom")),
            P(("iface", "dom")),
            P(("iface", "dom")),
            P(None, ("iface", "dom")),
            P(None, ("iface", "dom")),
        ),
        out_specs=(P(("iface", "dom")), P(("iface", "dom"))),
        check_vma=False,
    )
```

profile of v0, /device:TPU:0, one launch (start us, length us, event | category | flops | bytes accessed | tf_op | source)
XLA Modules:
  0.0 240.4 jit_solution(12346703330274250481)
XLA Ops:
  2.1 2.9 %collective-permute-start = (f32[1]{0:T(128)}, f32[1]{0:T(128)}, u32[]{:S(2)}, u32[]{:S(2)}) collective-permute-start(f32[1]{0:T(128)} %get-tuple-element.24), channel_id=1, source_target_pairs={{0,1},{1,2},{2,3},{3,4},{4,5},{5,6},{6,7},{7,8},{8,9},{9,10},{10,1... | collective-permute-start | bytes 20 | tf_op jit(solution)/shard_map/ppermute | solution.py:15
  6.3 3.4 %collective-permute-done.1 = f32[1]{0:T(128)} collective-permute-done((f32[1]{0:T(128)}, f32[1]{0:T(128)}, u32[]{:S(2)}, u32[]{:S(2)}) %collective-permute-start.1) | collective-permute-done | bytes 36 | tf_op jit(solution)/shard_map/ppermute | solution.py:15
  9.7 2.8 %fusion.70 = (f32[4096]{0:T(1024)}, f32[4096]{0:T(1024)S(1)}) fusion(f32[4096]{0:T(1024)} %param.9, f32[1]{0:T(128)} %collective-permute-done.1, f32[4096]{0:T(1024)} %param.7, f32[1]{0:T(128)} %collective-permute-done, f32[4096]{0:T(1024)} %param.10, f32[4096]{0:T(1024)} %param.11), kind=kLoop, calls=%fused_computation.102 | loop fusion | flops 32768 | bytes 98312 | tf_op jit(solution)/shard_map/sub | solution.py:46
  13.3 3.6 %fusion.19 = f32[101,101]{0,1:T(8,128)S(1)} fusion(f32[1,4096]{1,0:T(1,128)S(1)} %bitcast.102, f32[100,4096]{1,0:T(8,128)} %param.12), kind=kOutput, calls=%fused_computation.22 | convolution fusion | flops 501813248 | bytes 1695588 | tf_op jit(solution)/shard_map/dot_general | solution.py:48
  18.4 43.2 %all-reduce.2 = (f32[101,101]{0,1:T(8,128)S(1)}, f32[101]{0:T(128)S(1)}) all-reduce(f32[101,101]{0,1:T(8,128)S(1)} %fusion.19, f32[101]{0:T(128)S(1)} %fusion.29), channel_id=1, replica_groups=mesh['iface'=8,'dom'=4] {'iface','dom'}, use_global_device_ids=true, to_apply=%region_0.0 | all-reduce | flops 10302 | bytes 82416 | tf_op jit(solution)/shard_map/psum | solution.py:47
  62.4 10.1 %cholesky.44 = f32[101,101]{1,0:T(8,128)S(1)} custom-call(f32[101,101]{1,0:T(8,128)} %fusion.42), custom_call_target="Cholesky" | custom-call | tf_op jit(solution)/shard_map/jit(cholesky)/cholesky | solution.py:51
  74.5 8.5 %custom-call.30 = f32[1,101,101]{1,2,0:T(8,128)S(1)} custom-call(f32[1,101,101]{2,1,0:T(8,128)} %fusion.31), custom_call_target="InvertDiagBlocksLowerTriangular" | custom-call | tf_op jit(solution)/shard_map/jit(_cho_solve)/triangular_solve | solution.py:52
  83.4 1.7 fusion
  85.8 1.9 collective-permute-start.2
  89.1 3.7 %collective-permute-done.3 = f32[1]{0:T(128)} collective-permute-done((f32[1]{0:T(128)}, f32[1]{0:T(128)}, u32[]{:S(2)}, u32[]{:S(2)}) %collective-permute-start.3) | collective-permute-done | bytes 36 | tf_op jit(solution)/shard_map/ppermute | solution.py:15
  92.8 1.9 fusion.67
  94.7 2.1 fusion.21
  98.3 42.2 %all-reduce.1 = (f32[102,102]{0,1:T(8,128)S(1)}, f32[102]{0:T(128)S(1)}) all-reduce(f32[102,102]{0,1:T(8,128)} %fusion.21, f32[102]{0:T(128)S(1)} %fusion.28), channel_id=1, replica_groups=mesh['iface'=8,'dom'=4] {'iface','dom'}, use_global_device_ids=true, to_apply=%region_4.5 | all-reduce | flops 10506 | bytes 84048 | tf_op jit(solution)/shard_map/psum | solution.py:47
  141.3 10.2 %cholesky.86 = f32[102,102]{1,0:T(8,128)S(1)} custom-call(f32[102,102]{1,0:T(8,128)} %fusion.39), custom_call_target="Cholesky" | custom-call | tf_op jit(solution)/shard_map/jit(cholesky)/cholesky | solution.py:51
  153.4 8.6 %custom-call.31 = f32[1,102,102]{1,2,0:T(8,128)S(1)} custom-call(f32[1,102,102]{2,1,0:T(8,128)} %fusion.32), custom_call_target="InvertDiagBlocksLowerTriangular" | custom-call | tf_op jit(solution)/shard_map/jit(_cho_solve)/triangular_solve | solution.py:52
  162.4 1.7 fusion.4
  164.7 1.8 collective-permute-start.4
  167.9 3.9 %collective-permute-done.5 = f32[1]{0:T(128)} collective-permute-done((f32[1]{0:T(128)}, f32[1]{0:T(128)}, u32[]{:S(2)}, u32[]{:S(2)}) %collective-permute-start.5) | collective-permute-done | bytes 36 | tf_op jit(solution)/shard_map/ppermute | solution.py:15
  171.8 1.9 fusion.64
  173.7 1.5 fusion.30
  176.7 42.2 %all-reduce = (f32[103,103]{0,1:T(8,128)S(1)}, f32[103]{0:T(128)S(1)}) all-reduce(f32[103,103]{0,1:T(8,128)S(1)} %fusion.30, f32[103]{0:T(128)S(1)} %convolution_bitcast_fusion.2), channel_id=1, replica_groups=mesh['iface'=8,'dom'=4] {'iface','dom'}, use_global_device_ids=true, to_apply=%region_8.9 | all-reduce | flops 10712 | bytes 85696 | tf_op jit(solution)/shard_map/psum | solution.py:47
  219.0 9.4 %cholesky.96 = f32[103,103]{1,0:T(8,128)S(1)} custom-call(f32[103,103]{1,0:T(8,128)S(1)} %fusion.36), custom_call_target="Cholesky" | custom-call | tf_op jit(solution)/shard_map/jit(cholesky)/cholesky | solution.py:51
  229.8 7.9 %custom-call.32 = f32[1,103,103]{1,2,0:T(8,128)S(1)} custom-call(f32[1,103,103]{2,1,0:T(8,128)S(1)} %fusion.33), custom_call_target="InvertDiagBlocksLowerTriangular" | custom-call | tf_op jit(solution)/shard_map/jit(_cho_solve)/triangular_solve | solution.py:52
  238.1 1.7 fusion.10
  (73 shorter events, 20.4 us)
Async XLA Ops:
  0.6 16.3 %copy-start = (f32[100,4096]{1,0:T(8,128)S(1)}, f32[100,4096]{1,0:T(8,128)}, u32[]{:S(2)}) copy-start(f32[100,4096]{1,0:T(8,128)} %param.12) | copy-start | bytes 4915204
  2.1 4.2 %collective-permute-start = (f32[1]{0:T(128)}, f32[1]{0:T(128)}, u32[]{:S(2)}, u32[]{:S(2)}) collective-permute-start(f32[1]{0:T(128)} %get-tuple-element.24), channel_id=1, source_target_pairs={{0,1},{1,2},{2,3},{3,4},{4,5},{5,6},{6,7},{7,8},{8,9},{9,10},{10,1... | collective-permute-start | bytes 20 | tf_op jit(solution)/shard_map/ppermute | solution.py:15
  5.0 4.7 %collective-permute-start.1 = (f32[1]{0:T(128)}, f32[1]{0:T(128)}, u32[]{:S(2)}, u32[]{:S(2)}) collective-permute-start(f32[1]{0:T(128)} %get-tuple-element.25), channel_id=1, source_target_pairs={{1,0},{2,1},{3,2},{4,3},{5,4},{6,5},{7,6},{8,7},{9,8},{10,9},{11,1... | collective-permute-start | bytes 20 | tf_op jit(solution)/shard_map/ppermute | solution.py:15
  13.3 3.7 %copy-start.4 = (f32[4096]{0:T(1024)}, f32[4096]{0:T(1024)S(1)}, u32[]{:S(2)}) copy-start(f32[4096]{0:T(1024)S(1)} %get-tuple-element.19) | copy-start | bytes 49156
  13.3 5.1 %copy-start.2 = (f32[4096]{0:T(1024)}, f32[4096]{0:T(1024)S(1)}, u32[]{:S(2)}) copy-start(f32[4096]{0:T(1024)S(1)} %get-tuple-element.18) | copy-start | bytes 49156
  13.3 70.1 %copy-start.1 = (f32[100,4096]{1,0:T(8,128)S(1)}, f32[100,4096]{1,0:T(8,128)}, u32[]{:S(2)}) copy-start(f32[100,4096]{1,0:T(8,128)} %param.13) | copy-start | bytes 4915204
  62.4 30.4 %copy-start.6 = (f32[4096]{0:T(1024)S(1)}, f32[4096]{0:T(1024)}, u32[]{:S(2)}) copy-start(f32[4096]{0:T(1024)} %param.10) | copy-start | bytes 49156
  62.4 32.3 %copy-start.5 = (f32[4096]{0:T(1024)S(1)}, f32[4096]{0:T(1024)}, u32[]{:S(2)}) copy-start(f32[4096]{0:T(1024)} %copy-done.4) | copy-start | bytes 49156
  62.4 32.4 %copy-start.3 = (f32[4096]{0:T(1024)S(1)}, f32[4096]{0:T(1024)}, u32[]{:S(2)}) copy-start(f32[4096]{0:T(1024)} %copy-done.2) | copy-start | bytes 49156
  83.1 9.7 %copy-start.8 = (f32[4096]{0:T(1024)S(1)}, f32[4096]{0:T(1024)}, u32[]{:S(2)}) copy-start(f32[4096]{0:T(1024)} %param.11) | copy-start | bytes 49156
  85.8 3.3 %collective-permute-start.2 = (f32[1]{0:T(128)}, f32[1]{0:T(128)}, u32[]{:S(2)}, u32[]{:S(2)}) collective-permute-start(f32[1]{0:T(128)} %get-tuple-element.22), channel_id=1, source_target_pairs={{0,1},{1,2},{2,3},{3,4},{4,5},{5,6},{6,7},{7,8},{8,9},{9,10},{10,1... | collective-permute-start | bytes 20 | tf_op jit(solution)/shard_map/ppermute | solution.py:15
  87.6 5.2 %collective-permute-start.3 = (f32[1]{0:T(128)}, f32[1]{0:T(128)}, u32[]{:S(2)}, u32[]{:S(2)}) collective-permute-start(f32[1]{0:T(128)} %get-tuple-element.23), channel_id=1, source_target_pairs={{1,0},{2,1},{3,2},{4,3},{5,4},{6,5},{7,6},{8,7},{9,8},{10,9},{11,1... | collective-permute-start | bytes 20 | tf_op jit(solution)/shard_map/ppermute | solution.py:15
  94.7 2.1 copy-start.14
  94.7 3.6 %copy-start.11 = (f32[4096]{0:T(1024)}, f32[4096]{0:T(1024)S(1)}, u32[]{:S(2)}) copy-start(f32[4096]{0:T(1024)S(1)} %get-tuple-element.15) | copy-start | bytes 49156
  141.3 30.5 %copy-start.7 = (f32[4096]{0:T(1024)S(1)}, f32[4096]{0:T(1024)}, u32[]{:S(2)}) copy-start(f32[4096]{0:T(1024)} %param.10) | copy-start | bytes 49156
  141.3 30.5 %copy-start.9 = (f32[4096]{0:T(1024)S(1)}, f32[4096]{0:T(1024)}, u32[]{:S(2)}) copy-start(f32[4096]{0:T(1024)} %param.11) | copy-start | bytes 49156
  162.0 11.7 %copy-start.12 = (f32[4096]{0:T(1024)S(1)}, f32[4096]{0:T(1024)}, u32[]{:S(2)}) copy-start(f32[4096]{0:T(1024)} %copy-done.11) | copy-start | bytes 49156
  162.0 11.7 %copy-start.15 = (f32[4096]{0:T(1024)S(1)}, f32[4096]{0:T(1024)}, u32[]{:S(2)}) copy-start(f32[4096]{0:T(1024)} %copy-done.14) | copy-start | bytes 49156
  164.7 3.1 %collective-permute-start.4 = (f32[1]{0:T(128)}, f32[1]{0:T(128)}, u32[]{:S(2)}, u32[]{:S(2)}) collective-permute-start(f32[1]{0:T(128)} %get-tuple-element.20), channel_id=1, source_target_pairs={{0,1},{1,2},{2,3},{3,4},{4,5},{5,6},{6,7},{7,8},{8,9},{9,10},{10,1... | collective-permute-start | bytes 20 | tf_op jit(solution)/shard_map/ppermute | solution.py:15
  166.6 5.2 %collective-permute-start.5 = (f32[1]{0:T(128)}, f32[1]{0:T(128)}, u32[]{:S(2)}, u32[]{:S(2)}) collective-permute-start(f32[1]{0:T(128)} %get-tuple-element.21), channel_id=1, source_target_pairs={{1,0},{2,1},{3,2},{4,3},{5,4},{6,5},{7,6},{8,7},{9,8},{10,9},{11,1... | collective-permute-start | bytes 20 | tf_op jit(solution)/shard_map/ppermute | solution.py:15
  173.7 3.0 %copy-start.16 = (f32[4096]{0:T(1024)}, f32[4096]{0:T(1024)S(1)}, u32[]{:S(2)}) copy-start(f32[4096]{0:T(1024)S(1)} %get-tuple-element.11) | copy-start | bytes 49156
  175.2 62.8 %copy-start.10 = (f32[4096]{0:T(1024)S(1)}, f32[4096]{0:T(1024)}, u32[]{:S(2)}) copy-start(f32[4096]{0:T(1024)} %get-tuple-element.16) | copy-start | bytes 49156
  175.3 62.8 %copy-start.13 = (f32[4096]{0:T(1024)S(1)}, f32[4096]{0:T(1024)}, u32[]{:S(2)}) copy-start(f32[4096]{0:T(1024)} %get-tuple-element.12) | copy-start | bytes 49156
where the time goes:
time: 242 us; the launch traced here: 240 us
  blocking collectives  128 us (53%)
  other arithmetic  69.4 us (29%)
  matrix products  17.6 us (7%)
  waiting for transfers between devices  11 us (5%)
  starting transfers between devices  10.6 us (4%)
  local copies, waits for them, and re-layouts  3.08 us (1%)
    psum x3, blocking collectives, shards(): lax.psum((jnp.dot(hist_v, hist_v.T, precision=high), jnp.dot(hist_v, resi...  128 us
    another operation x9, other arithmetic, shards(): factor = jnp.linalg.cholesky(gram_matrix)  31.8 us
    another operation x6, other arithmetic, shards(): coeffs = -jax.scipy.linalg.cho_solve((factor, True), projection)  28.3 us
    ppermute x6, waiting for transfers between devices, from_behind(): lax.ppermute(value, axis, [(source, source + steps) for source in range(i...  11 us
    ppermute x6, starting transfers between devices, from_behind(): lax.ppermute(value, axis, [(source, source + steps) for source in range(i...  10.6 us
    dot_general x3, matrix products, shards(): jnp.dot(hist_v, hist_v.T, precision=high)  7.23 us
    sub x3, other arithmetic, shards(): estimate - old_estimate  6.7 us
    dot_general x3, matrix products, shards(): current = estimate + jnp.dot(coeffs, hist_w, precision=high)  5.13 us
  transfers between devices with their start and end apart: 6, of which 3 were waited for; matrix products, arithmetic and copies ran while one was open for 0% of the time, Pallas kernels for 0%

commit v1 on v0

v1 whole, which is shorter than its diff:
```python
import functools
import jax
import jax.numpy as jnp
from jax import lax
from jax.experimental import pallas as pl
from jax.experimental.pallas import tpu as pltpu
from jax.sharding import PartitionSpec as P

ITERS = 3
coupling = 0.25
LANES = 128
AXES = ("iface", "dom")
F32 = jnp.float32


def invert(matrix, rows):
    lane8 = lax.broadcasted_iota(jnp.int32, (8, LANES), 1)
    sub8 = lax.broadcasted_iota(jnp.int32, (8, LANES), 0)
    blocks = [matrix[8 * at : 8 * at + 8, :] for at in range(rows // 8)]
    for step in range(rows // 8):
        first = 8 * step
        inside = (lane8 >= first) & (lane8 < first + 8)
        unit = (lane8 - first == sub8).astype(F32)
        pivots = blocks[step]
        columns = [jnp.broadcast_to(pivots[:, first + at : first + at + 1], (8, LANES)) for at in range(8)]
        panel = jnp.where(inside, unit, pivots)
        for at in range(8):
            inverse = 1.0 / columns[at][at : at + 1, :]
            own = sub8 == at
            factor = columns[at]
            row = panel[at : at + 1, :] * inverse
            panel = jnp.where(own, row, panel - factor * row)
            for later in range(at + 1, 8):
                row = columns[later][at : at + 1, :] * inverse
                columns[later] = jnp.where(own, row, columns[later] - factor * row)
        for other in range(rows // 8):
            if other != step:
                block = blocks[other]
                total = jnp.where(inside, 0.0, block)
                for at in range(8):
                    column = jnp.broadcast_to(block[:, first + at : first + at + 1], (8, LANES))
                    total = total - column * panel[at : at + 1, :]
                blocks[other] = total
        blocks[step] = panel
    return jnp.concatenate(blocks, axis=0)


def kernel(
    sizes,
    interface,
    previous_residual,
    previous_estimate,
    forcing,
    stiffness,
    history_residual,
    history_estimate,
    next_ref,
    last_ref,
    cur_x,
    est_x,
    force_x,
    stiff_x,
    old_res,
    hist_v,
    hist_w,
    new_v,
    new_w,
    dots_in,
    square,
    part_out,
    part_in,
    gathered,
    row_in,
    load_sem,
    halo_sem,
    wide_sem,
    part_sem,
    gather_sem,
    row_sem,
):
    n_iface, n_dom, hist, base, rows, width, share = sizes
    count = n_iface * n_dom
    me = lax.axis_index("iface") * n_dom + lax.axis_index("dom")
    full = width + 2 * LANES

    def place(index):
        return (index // n_dom, lax.rem(index, n_dom))

    def peer(step):
        return lax.rem(me + step, count)

    barrier = pltpu.get_barrier_semaphore()

    @pl.loop(1, count)
    def _(step):
        pl.semaphore_signal(barrier, inc=1, device_id=place(peer(step)), device_id_type=pl.DeviceIdType.MESH)

    own = pl.ds(LANES, width)
    load_v = pltpu.make_async_copy(history_residual, hist_v, load_sem.at[0])
    load_v.start()
    small = []
    for at, (source, target) in enumerate(
        [
            (interface, cur_x.at[:, own]),
            (previous_estimate, est_x.at[:, own]),
            (forcing, force_x.at[:, own]),
            (stiffness, stiff_x.at[:, own]),
            (previous_residual, old_res),
        ]
    ):
        copy = pltpu.make_async_copy(source, target, load_sem.at[2 + at])
        copy.start()
        small.append(copy)
    load_w = pltpu.make_async_copy(history_estimate, hist_w.at[:, own], load_sem.at[1])
    load_w.start()
    new_v[...] = jnp.zeros(new_v.shape, F32)
    new_w[...] = jnp.zeros(new_w.shape, F32)

    load_v.wait()
    depth = 512

    def add_gram(at, total):
        block = hist_v[:, pl.ds(pl.multiple_of(at * depth, depth), depth)]
        return total + lax.dot_general(
            block, block, (((1,), (1,)), ((), ())), precision=lax.Precision.HIGHEST, preferred_element_type=F32
        )

    gram = lax.fori_loop(0, width // depth, add_gram, jnp.zeros((hist, hist), F32))
    square[...] = jnp.zeros(square.shape, F32)
    square[0:hist, 0:hist] = gram
    for at in range(count):
        part_out[at] = square[at * share : (at + 1) * share, :]
    part_in[me] = part_out[me]
    for copy in small:
        copy.wait()
    load_w.wait()
    pl.semaphore_wait(barrier, count - 1)

    halos = []
    right, left = place(peer(1)), place(peer(count - 1))
    for at, ref in enumerate([cur_x, est_x, force_x, stiff_x]):
        for side, (source, target, device) in enumerate([(width, 0, right), (LANES, width + LANES, left)]):
            copy = pltpu.make_async_remote_copy(
                src_ref=ref.at[:, pl.ds(source, LANES)],
                dst_ref=ref.at[:, pl.ds(target, LANES)],
                send_sem=halo_sem.at[0, at, side],
                recv_sem=halo_sem.at[1, at, side],
                device_id=device,
                device_id_type=pl.DeviceIdType.MESH,
            )
            copy.start()
            halos.append(copy)

    def exchange(source_of, target, sems):
        def send(step):
            to = peer(step)
            return pltpu.make_async_remote_copy(
                src_ref=source_of(to),
                dst_ref=target.at[me],
                send_sem=sems.at[0],
                recv_sem=sems.at[1],
                device_id=place(to),
                device_id_type=pl.DeviceIdType.MESH,
            )

        @pl.loop(1, count)
        def _(step):
            send(step).start()

    def arrive(target, sems):
        most = target.at[pl.ds(0, count - 1)]
        pltpu.make_async_copy(most, most, sems.at[1]).wait()
        pltpu.make_async_copy(most, most, sems.at[0]).wait()

    exchange(lambda to: part_out.at[to], part_in, part_sem)
    wide = []
    for side, (source, target, device) in enumerate([(width, 0, right), (LANES, width + LANES, left)]):
        copy = pltpu.make_async_remote_copy(
            src_ref=hist_w.at[:, pl.ds(source, LANES)],
            dst_ref=hist_w.at[:, pl.ds(target, LANES)],
            send_sem=wide_sem.at[0, side],
            recv_sem=wide_sem.at[1, side],
            device_id=device,
            device_id_type=pl.DeviceIdType.MESH,
        )
        copy.start()
        wide.append(copy)
    for copy in halos:
        copy.wait()

    lane = lax.broadcasted_iota(jnp.int32, (1, full), 1)
    outside = ((me == 0) & (lane < LANES)) | ((me == count - 1) & (lane >= LANES + width))
    eye = (
        lax.broadcasted_iota(jnp.int32, (rows, LANES), 0) == lax.broadcasted_iota(jnp.int32, (rows, LANES), 1)
    ).astype(F32)
    row_at = lax.broadcasted_iota(jnp.int32, (rows, LANES), 0)
    ones = jnp.ones((8, LANES), F32)
    cur_x[...] = jnp.where(outside, 0.0, cur_x[...])

    def column_of(row):
        return jnp.broadcast_to(jnp.sum(eye * row, axis=1, keepdims=True), (rows, LANES))

    def over_rows(value):
        return jnp.sum(value, axis=0, keepdims=True)

    def begin(iteration):
        current = cur_x[...]
        before = pltpu.roll(current, 1, 1)
        after = pltpu.roll(current, full - 1, 1)
        estimate = force_x[...] + stiff_x[...] * jnp.tanh(current) + coupling * (before + after)
        residual = (estimate - current)[:, LANES : LANES + width]
        new_w[iteration : iteration + 1, :] = estimate - est_x[...]
        est_x[...] = estimate
        new_v[iteration : iteration + 1, :] = residual - old_res[...]
        old_res[...] = residual

        def add(at, totals):
            span = pl.ds(pl.multiple_of(at * LANES, LANES), LANES)
            block, extra = hist_v[:, span], new_v[:, span]
            res, new = old_res[:, span], new_v[iteration : iteration + 1, span]
            return (totals[0] + block * res, totals[1] + block * new, totals[2] + extra * res, totals[3] + extra * new)

        zero, few = jnp.zeros((hist, LANES), F32), jnp.zeros((8, LANES), F32)
        totals = lax.fori_loop(0, width // LANES, add, (zero, zero, few, few), unroll=4)
        dots_in[iteration] = jnp.zeros((2, LANES), F32)
        for which in range(4):
            sums = lax.dot_general(
                ones, totals[which], (((1,), (1,)), ((), ())), precision=lax.Precision.HIGHEST, preferred_element_type=F32
            )
            if which < 2:
                dots_in[iteration, which : which + 1, 0:hist] = sums[0:1, :]
            else:
                dots_in[iteration, which - 2 : which - 1, base : base + 8] = sums[0:1, :]
        row_in[iteration, me] = dots_in[iteration]
        exchange(lambda to: dots_in.at[iteration], row_in.at[iteration], row_sem.at[iteration])

    def sums_of(iteration):
        arrive(row_in.at[iteration], row_sem.at[iteration])
        return jnp.sum(row_in[iteration], axis=0)

    begin(0)

    arrive(part_in, part_sem)
    gathered[me] = jnp.sum(part_in[...], axis=0)
    exchange(lambda to: gathered.at[me], gathered, gather_sem)
    arrive(gathered, gather_sem)
    for at in range(-(-base // share)):
        square[at * share : (at + 1) * share, :] = gathered[at]
    kept = (row_at < hist) & (lax.broadcasted_iota(jnp.int32, (rows, LANES), 1) < hist)
    square[0:rows, :] = jnp.where(kept, square[0:rows, :], eye)
    square[0:base, :] = invert(square, base)
    square[0:rows, :] = jnp.where(kept, square[0:rows, :], 0.0)
    for copy in wide:
        copy.wait()

    solved, columns = [], []
    for iteration in range(ITERS):
        both = sums_of(iteration)
        proj, new = both[0:1, :], both[1:2, :]
        inverse = square[0:rows, :]
        proj_col, new_col = column_of(proj), column_of(new)
        proj_sol = jnp.broadcast_to(jnp.sum(inverse * proj, axis=1, keepdims=True), (rows, LANES))
        new_sol = jnp.broadcast_to(jnp.sum(inverse * new, axis=1, keepdims=True), (rows, LANES))
        solved.append(new_sol)
        columns.append(new_col)
        size = iteration + 1
        schur = [
            [columns[a][base + b : base + b + 1, :] - over_rows(columns[a] * solved[b]) for b in range(a + 1)]
            for a in range(size)
        ]
        right_side = [proj_col[base + a : base + a + 1, :] - over_rows(columns[a] * proj_sol) for a in range(size)]
        for a in range(size):
            for b in range(a + 1, size):
                factor = schur[b][a] / schur[a][a]
                right_side[b] = right_side[b] - factor * right_side[a]
                for c in range(a + 1, b + 1):
                    schur[b][c] = schur[b][c] - factor * schur[c][a]
        answer = [None] * size
        for a in reversed(range(size)):
            value = right_side[a]
            for b in range(a + 1, size):
                value = value - schur[b][a] * answer[b]
            answer[a] = value / schur[a][a]
        weights = proj_sol
        for a in range(size):
            weights = jnp.where(row_at == base + a, answer[a], weights - solved[a] * answer[a])

        def combine(at, carry):
            span = pl.ds(pl.multiple_of(at * LANES, LANES), LANES)
            cur_x[:, span] = (
                est_x[:, span]
                - over_rows(hist_w[:, span] * weights[0:hist, :])
                - over_rows(new_w[:, span] * weights[base:rows, :])
            )
            return carry

        lax.fori_loop(0, full // LANES, combine, 0, unroll=2)
        if iteration + 1 < ITERS:
            cur_x[...] = jnp.where(outside, 0.0, cur_x[...])
            begin(iteration + 1)
    next_ref[...] = cur_x[:, LANES : LANES + width]
    last_ref[...] = old_res[...]


def shards(n_iface, n_dom, *args):
    width = args[0].shape[0]
    hist = args[5].shape[0]
    base = -(-hist // 8) * 8
    rows = base + 8
    count = n_iface * n_dom
    share = -(-base // count)
    full = width + 2 * LANES
    vectors = [a.reshape(1, width) for a in args[:5]]
    any_spec = pl.BlockSpec(memory_space=pl.ANY)
    vmem_spec = pl.BlockSpec(memory_space=pltpu.VMEM)
    outs = pl.pallas_call(
        functools.partial(kernel, (n_iface, n_dom, hist, base, rows, width, share)),
        out_shape=[jax.ShapeDtypeStruct((1, width), F32)] * 2,
        in_specs=[any_spec] * 7,
        out_specs=[vmem_spec] * 2,
        scratch_shapes=[
            pltpu.VMEM((1, full), F32),
            pltpu.VMEM((1, full), F32),
            pltpu.VMEM((1, full), F32),
            pltpu.VMEM((1, full), F32),
            pltpu.VMEM((1, width), F32),
            pltpu.VMEM((hist, width), F32),
            pltpu.VMEM((hist, full), F32),
            pltpu.VMEM((8, width), F32),
            pltpu.VMEM((8, full), F32),
            pltpu.VMEM((ITERS, 2, LANES), F32),
            pltpu.VMEM((max(LANES, share * count), LANES), F32),
            pltpu.VMEM((count, share, LANES), F32),
            pltpu.VMEM((count, share, LANES), F32),
            pltpu.VMEM((count, share, LANES), F32),
            pltpu.VMEM((ITERS, count, 2, LANES), F32),
            pltpu.SemaphoreType.DMA((7,)),
            pltpu.SemaphoreType.DMA((2, 4, 2)),
            pltpu.SemaphoreType.DMA((2, 2)),
            pltpu.SemaphoreType.DMA((2,)),
            pltpu.SemaphoreType.DMA((2,)),
            pltpu.SemaphoreType.DMA((ITERS, 2)),
        ],
        compiler_params=pltpu.CompilerParams(collective_id=0, has_side_effects=True),
        name="coupling",
    )(*vectors, args[5], args[6])
    return outs[0].reshape(width), outs[1].reshape(width)


def solution(mesh):
    one = P(AXES)
    return jax.shard_map(
        functools.partial(shards, mesh.shape["iface"], mesh.shape["dom"]),
        mesh=mesh,
        in_specs=(one,) * 5 + (P(None, AXES),) * 2,
        out_specs=(one, one),
        check_vma=False,
    )
```

time: 242 us -> 37.1 us (0.15)
  blocking collectives: 128 us -> 0 us
  other arithmetic: 69.4 us -> 0 us
  Pallas kernels: 0 us -> 33.5 us
  matrix products: 17.6 us -> 0 us
  waiting for transfers between devices: 11 us -> 0 us
  starting transfers between devices: 10.6 us -> 0 us
    psum x3 -> x0, blocking collectives: 128 us -> none  [shards(): lax.psum((jnp.dot(hist_v, hist_v.T, precision=high), jnp.dot(hist_v, resi...]
    another operation x15 -> x0, other arithmetic: 60.1 us -> none  [the longest x9 31.8 us: shards(): factor = jnp.linalg.cholesky(gram_matrix)]
    pallas_call x0 -> x1, Pallas kernels: none -> 33.5 us  [shards(): pl.pallas_call(functools.partial(kernel, (n_iface, n_dom, hist, base, row...]
    dot_general x9 -> x0, matrix products: 16.6 us -> none  [the longest x3 7.23 us: shards(): jnp.dot(hist_v, hist_v.T, precision=high)]
    ppermute x6 -> x0, waiting for transfers between devices: 11 us -> none  [from_behind(): lax.ppermute(value, axis, [(source, source + steps) for source in range(i...]
    ppermute x6 -> x0, starting transfers between devices: 10.6 us -> none  [from_behind(): lax.ppermute(value, axis, [(source, source + steps) for source in range(i...]
    sub x6 -> x0, other arithmetic: 7.45 us -> none  [the longest x3 6.7 us: shards(): estimate - old_estimate]
    slice x3 -> x0, local copies, waits for them, and re-layouts: 2.69 us -> none  [solver_map(): from_left = from_behind(current[-1:], ('iface', 'dom'), 1)]
  transfers between devices with their start and end apart: 6 -> 0, of which waited for: 3 -> 0; matrix products, arithmetic and copies ran while one was open for 0% -> 0% of each run, Pallas kernels for 0% -> 0%
where the time goes in v1:
time: 37.1 us; the launch traced here: 36.8 us
  Pallas kernels  33.5 us (90%)
  local copies, waits for them, and re-layouts  2.65 us (7%)
  between operations  0.64 us (2%)
    pallas_call x1, Pallas kernels, shards(): pl.pallas_call(functools.partial(kernel, (n_iface, n_dom, hist, base, row...  33.5 us
    unnamed x2, local copies, waits for them, and re-layouts  2.65 us

profile of v1, /device:TPU:0, one launch (start us, length us, event | category | flops | bytes accessed | tf_op | source)
XLA Modules:
  0.0 36.8 jit_solution(4704779434275058328)
XLA Ops:
  0.6 33.5 %coupling.1 = (f32[1,4096]{1,0:T(1,128)}, f32[1,4096]{1,0:T(1,128)}) custom-call(f32[1,4096]{1,0:T(1,128)} %bitcast.7, f32[1,4096]{1,0:T(1,128)} %bitcast.8, f32[1,4096]{1,0:T(1,128)} %bitcast.9, f32[1,4096]{1,0:T(1,128)} %bitcast.10, f32[1,4096]{1,0:T(1,128)} %bitcast.11, f32[100,4096]{1,0:T(8,128)} %history_residual.1, f32[100,4096]{1,0:T(8,128)} %history_estimate.1), custom_call_target="tpu_custom_call" | custom-call | tf_op jit(solution)/shard_map/coupling/pallas_call | solution.py:316
  34.1 1.3 %copy.11 = f32[4096]{0:T(1024)} copy(f32[4096]{0:T(1024)} %bitcast.13) | data formatting | bytes 32768
  35.5 1.3 %copy.12 = f32[4096]{0:T(1024)} copy(f32[4096]{0:T(1024)} %bitcast.12) | data formatting | bytes 32768

commit v2 on v1

--- a/solution.py
+++ b/solution.py
@@ -69,35 +69,43 @@
     square,
     part_out,
     part_in,
+    mid_in,
     gathered,
     row_in,
+    piece_sem,
     load_sem,
     halo_sem,
     wide_sem,
     part_sem,
+    mid_sem,
     gather_sem,
     row_sem,
 ):
-    n_iface, n_dom, hist, base, rows, width, share = sizes
+    n_iface, n_dom, hist, base, rows, width, share, depth = sizes
     count = n_iface * n_dom
-    me = lax.axis_index("iface") * n_dom + lax.axis_index("dom")
+    at_iface, at_dom = lax.axis_index("iface"), lax.axis_index("dom")
+    me = at_iface * n_dom + at_dom
+    last = count - 1
     full = width + 2 * LANES
+    ifaces = [lax.rem(at_iface + step, n_iface) for step in range(n_iface)]
+    doms = [lax.rem(at_dom + step, n_dom) for step in range(n_dom)]
+    everyone = [(a, b) for a in ifaces for b in doms][1:]
 
     def place(index):
         return (index // n_dom, lax.rem(index, n_dom))
 
-    def peer(step):
-        return lax.rem(me + step, count)
-
     barrier = pltpu.get_barrier_semaphore()
-
-    @pl.loop(1, count)
-    def _(step):
-        pl.semaphore_signal(barrier, inc=1, device_id=place(peer(step)), device_id_type=pl.DeviceIdType.MESH)
+    for device in everyone:
+        pl.semaphore_signal(barrier, inc=1, device_id=device, device_id_type=pl.DeviceIdType.MESH)
 
     own = pl.ds(LANES, width)
-    load_v = pltpu.make_async_copy(history_residual, hist_v, load_sem.at[0])
-    load_v.start()
+
+    def piece(at):
+        span = pl.ds(pl.multiple_of(at * depth, depth), depth)
+        return pltpu.make_async_copy(history_residual.at[:, span], hist_v.at[:, span], piece_sem.at[at])
+
+    for at in range(width // depth):
+        piece(at).start()
     small = []
     for at, (source, target) in enumerate(
         [
@@ -108,85 +116,104 @@
             (previous_residual, old_res),
         ]
     ):
-        copy = pltpu.make_async_copy(source, target, load_sem.at[2 + at])
+        copy = pltpu.make_async_copy(source, target, load_sem.at[1 + at])
         copy.start()
         small.append(copy)
-    load_w = pltpu.make_async_copy(history_estimate, hist_w.at[:, own], load_sem.at[1])
-    load_w.start()
+    load_w = pltpu.make_async_copy(history_estimate, hist_w.at[:, own], load_sem.at[0])
     new_v[...] = jnp.zeros(new_v.shape, F32)
     new_w[...] = jnp.zeros(new_w.shape, F32)
 
-    load_v.wait()
-    depth = 512
-
     def add_gram(at, total):
+        piece(at).wait()
         block = hist_v[:, pl.ds(pl.multiple_of(at * depth, depth), depth)]
         return total + lax.dot_general(
             block, block, (((1,), (1,)), ((), ())), precision=lax.Precision.HIGHEST, preferred_element_type=F32
         )
 
     gram = lax.fori_loop(0, width // depth, add_gram, jnp.zeros((hist, hist), F32))
+    load_w.start()
     square[...] = jnp.zeros(square.shape, F32)
     square[0:hist, 0:hist] = gram
-    for at in range(count):
-        part_out[at] = square[at * share : (at + 1) * share, :]
-    part_in[me] = part_out[me]
+    lane8 = lax.broadcasted_iota(jnp.int32, (8, LANES), 1)
+    blocks = (base // 8 + 1) // 2 * 2
+    pairs = blocks // 2
+
+    def natural(block):
+        return (lane8 >= 8 * block) & (lane8 < 8 * blocks)
+
+    for pair in range(n_dom * share):
+        where = (pair // share, pl.ds(8 * (pair % share), 8), slice(None))
+        if pair < pairs:
+            other = blocks - 1 - pair
+            moved = pltpu.roll(square[8 * other : 8 * other + 8, :], 8 * pair + 8, 1)
+            part_out[where] = jnp.where(natural(pair), square[8 * pair : 8 * pair + 8, :], moved)
+        else:
+            part_out[where] = jnp.zeros((8, LANES), F32)
+    part_in[at_dom] = part_out[at_dom]
     for copy in small:
         copy.wait()
-    load_w.wait()
-    pl.semaphore_wait(barrier, count - 1)
-
-    halos = []
-    right, left = place(peer(1)), place(peer(count - 1))
-    for at, ref in enumerate([cur_x, est_x, force_x, stiff_x]):
-        for side, (source, target, device) in enumerate([(width, 0, right), (LANES, width + LANES, left)]):
-            copy = pltpu.make_async_remote_copy(
-                src_ref=ref.at[:, pl.ds(source, LANES)],
-                dst_ref=ref.at[:, pl.ds(target, LANES)],
-                send_sem=halo_sem.at[0, at, side],
-                recv_sem=halo_sem.at[1, at, side],
-                device_id=device,
-                device_id_type=pl.DeviceIdType.MESH,
-            )
-            copy.start()
-            halos.append(copy)
-
-    def exchange(source_of, target, sems):
-        def send(step):
-            to = peer(step)
-            return pltpu.make_async_remote_copy(
-                src_ref=source_of(to),
-                dst_ref=target.at[me],
-                send_sem=sems.at[0],
-                recv_sem=sems.at[1],
-                device_id=place(to),
-                device_id_type=pl.DeviceIdType.MESH,
-            )
-
-        @pl.loop(1, count)
-        def _(step):
-            send(step).start()
-
-    def arrive(target, sems):
-        most = target.at[pl.ds(0, count - 1)]
+    pl.semaphore_wait(barrier, last)
+
+    right = place(lax.rem(me + 1, count))
+    left = place(lax.rem(me + last, count))
+
+    def edges(refs, sems):
+        copies = []
+        for at, ref in enumerate(refs):
+            for side, (source, target, device) in enumerate([(width, 0, right), (LANES, width + LANES, left)]):
+                copies.append(
+                    pltpu.make_async_remote_copy(
+                        src_ref=ref.at[:, pl.ds(source, LANES)],
+                        dst_ref=ref.at[:, pl.ds(target, LANES)],
+                        send_sem=sems.at[0, at, side],
+                        recv_sem=sems.at[1, at, side],
+                        device_id=device,
+                        device_id_type=pl.DeviceIdType.MESH,
+                    )
+                )
+        return copies[0::2], copies[1::2]
+
+    def edges_start(copies):
+        for side, some in enumerate([me < last, me > 0]):
+
+            @pl.when(some)
+            def _():
+                for copy in copies[side]:
+                    copy.start()
+
+    def edges_wait(copies):
+        for side, (sent, received) in enumerate([(me < last, me > 0), (me > 0, me < last)]):
+
+            @pl.when(sent)
+            def _():
+                for copy in copies[side]:
+                    copy.wait_send()
+
+            @pl.when(received)
+            def _():
+                for copy in copies[side]:
+                    copy.wait_recv()
+
+    def send(source, target, sems, device):
+        pltpu.make_async_remote_copy(
+            src_ref=source,
+            dst_ref=target,
+            send_sem=sems.at[0],
+            recv_sem=sems.at[1],
+            device_id=device,
+            device_id_type=pl.DeviceIdType.MESH,
+        ).start()
+
+    def arrive(target, many, sems):
+        most = target.at[pl.ds(0, many)]
         pltpu.make_async_copy(most, most, sems.at[1]).wait()
         pltpu.make_async_copy(most, most, sems.at[0]).wait()
 
-    exchange(lambda to: part_out.at[to], part_in, part_sem)
-    wide = []
-    for side, (source, target, device) in enumerate([(width, 0, right), (LANES, width + LANES, left)]):
-        copy = pltpu.make_async_remote_copy(
-            src_ref=hist_w.at[:, pl.ds(source, LANES)],
-            dst_ref=hist_w.at[:, pl.ds(target, LANES)],
-            send_sem=wide_sem.at[0, side],
-            recv_sem=wide_sem.at[1, side],
-            device_id=device,
-            device_id_type=pl.DeviceIdType.MESH,
-        )
-        copy.start()
-        wide.append(copy)
-    for copy in halos:
-        copy.wait()
+    for dom in doms[1:]:
+        send(part_out.at[dom], part_in.at[at_dom], part_sem, (at_iface, dom))
+    halos = edges([cur_x, est_x, force_x, stiff_x], halo_sem)
+    edges_start(halos)
+    wide = edges([hist_w], wide_sem)
 
     lane = lax.broadcasted_iota(jnp.int32, (1, full), 1)
     outside = ((me == 0) & (lane < LANES)) | ((me == count - 1) & (lane >= LANES + width))
@@ -195,7 +222,6 @@
     ).astype(F32)
     row_at = lax.broadcasted_iota(jnp.int32, (rows, LANES), 0)
     ones = jnp.ones((8, LANES), F32)
-    cur_x[...] = jnp.where(outside, 0.0, cur_x[...])
 
     def column_of(row):
         return jnp.broadcast_to(jnp.sum(eye * row, axis=1, keepdims=True), (rows, LANES))
@@ -232,26 +258,42 @@
             else:
                 dots_in[iteration, which - 2 : which - 1, base : base + 8] = sums[0:1, :]
         row_in[iteration, me] = dots_in[iteration]
-        exchange(lambda to: dots_in.at[iteration], row_in.at[iteration], row_sem.at[iteration])
+        for device in everyone:
+            send(dots_in.at[iteration], row_in.at[iteration, me], row_sem.at[iteration], device)
 
     def sums_of(iteration):
-        arrive(row_in.at[iteration], row_sem.at[iteration])
+        arrive(row_in.at[iteration], last, row_sem.at[iteration])
         return jnp.sum(row_in[iteration], axis=0)
 
+    arrive(part_in, n_dom - 1, part_sem)
+    mid_in[at_iface] = jnp.sum(part_in[...], axis=0)
+    for iface in ifaces[1:]:
+        send(mid_in.at[at_iface], mid_in.at[at_iface], mid_sem, (iface, at_dom))
+    edges_wait(halos)
+    cur_x[...] = jnp.where(outside, 0.0, cur_x[...])
     begin(0)
-
-    arrive(part_in, part_sem)
-    gathered[me] = jnp.sum(part_in[...], axis=0)
-    exchange(lambda to: gathered.at[me], gathered, gather_sem)
-    arrive(gathered, gather_sem)
-    for at in range(-(-base // share)):
-        square[at * share : (at + 1) * share, :] = gathered[at]
+    load_w.wait()
+    edges_start(wide)
+    arrive(mid_in, n_iface - 1, mid_sem)
+    gathered[at_dom] = jnp.sum(mid_in[...], axis=0)
+    for dom in doms[1:]:
+        send(gathered.at[at_dom], gathered.at[at_dom], gather_sem, (at_iface, dom))
+    arrive(gathered, n_dom - 1, gather_sem)
+    for pair in range(pairs):
+        other = blocks - 1 - pair
+        packed = gathered[pair // share, pl.ds(8 * (pair % share), 8), :]
+        square[8 * pair : 8 * pair + 8, :] = jnp.where(natural(pair), packed, 0.0)
+        moved = pltpu.roll(packed, LANES - 8 * pair - 8, 1)
+        square[8 * other : 8 * other + 8, :] = jnp.where(natural(other), moved, 0.0)
+    upper = square[...]
+    lane_block = lax.broadcasted_iota(jnp.int32, (LANES, LANES), 1) // 8
+    row_block = lax.broadcasted_iota(jnp.int32, (LANES, LANES), 0) // 8
+    square[...] = jnp.where(lane_block >= row_block, upper, upper.T)
     kept = (row_at < hist) & (lax.broadcasted_iota(jnp.int32, (rows, LANES), 1) < hist)
     square[0:rows, :] = jnp.where(kept, square[0:rows, :], eye)
     square[0:base, :] = invert(square, base)
     square[0:rows, :] = jnp.where(kept, square[0:rows, :], 0.0)
-    for copy in wide:
-        copy.wait()
+    edges_wait(wide)
 
     solved, columns = [], []
     for iteration in range(ITERS):
@@ -308,14 +350,17 @@
     base = -(-hist // 8) * 8
     rows = base + 8
     count = n_iface * n_dom
-    share = -(-base // count)
+    pairs = (base // 8 + 1) // 2
+    share = -(-pairs // n_dom)
+    depth = next(d for d in (512, 256, 128) if width % d == 0)
+    assert hist <= 112
     full = width + 2 * LANES
     vectors = [a.reshape(1, width) for a in args[:5]]
     any_spec = pl.BlockSpec(memory_space=pl.ANY)
     vmem_spec = pl.BlockSpec(memory_space=pltpu.VMEM)
     outs = pl.pallas_call(
-        functools.partial(kernel, (n_iface, n_dom, hist, base, rows, width, share)),
-        out_shape=[jax.ShapeDtypeStruct((1, width), F32)] * 2,
+        functools.partial(kernel, (n_iface, n_dom, hist, base, rows, width, share, depth)),
+        out_shape=[pltpu.VMEM((1, width), F32)] * 2,
         in_specs=[any_spec] * 7,
         out_specs=[vmem_spec] * 2,
         scratch_shapes=[
@@ -329,14 +374,17 @@
             pltpu.VMEM((8, width), F32),
             pltpu.VMEM((8, full), F32),
             pltpu.VMEM((ITERS, 2, LANES), F32),
-            pltpu.VMEM((max(LANES, share * count), LANES), F32),
-            pltpu.VMEM((count, share, LANES), F32),
-            pltpu.VMEM((count, share, LANES), F32),
-            pltpu.VMEM((count, share, LANES), F32),
+            pltpu.VMEM((LANES, LANES), F32),
+            pltpu.VMEM((n_dom, 8 * share, LANES), F32),
+            pltpu.VMEM((n_dom, 8 * share, LANES), F32),
+            pltpu.VMEM((n_iface, 8 * share, LANES), F32),
+            pltpu.VMEM((n_dom, 8 * share, LANES), F32),
             pltpu.VMEM((ITERS, count, 2, LANES), F32),
-            pltpu.SemaphoreType.DMA((7,)),
+            pltpu.SemaphoreType.DMA((width // depth,)),
+            pltpu.SemaphoreType.DMA((6,)),
             pltpu.SemaphoreType.DMA((2, 4, 2)),
-            pltpu.SemaphoreType.DMA((2, 2)),
+            pltpu.SemaphoreType.DMA((2, 1, 2)),
+            pltpu.SemaphoreType.DMA((2,)),
             pltpu.SemaphoreType.DMA((2,)),
             pltpu.SemaphoreType.DMA((2,)),
             pltpu.SemaphoreType.DMA((ITERS, 2)),
@@ -344,6 +392,22 @@
         compiler_params=pltpu.CompilerParams(collective_id=0, has_side_effects=True),
         name="coupling",
     )(*vectors, args[5], args[6])
+
+    def finish(a, b, c, d, sems):
+        copies = [pltpu.make_async_copy(a, c, sems.at[0]), pltpu.make_async_copy(b, d, sems.at[1])]
+        for copy in copies:
+            copy.start()
+        for copy in copies:
+            copy.wait()
+
+    outs = pl.pallas_call(
+        finish,
+        out_shape=[jax.ShapeDtypeStruct((1, width), F32)] * 2,
+        in_specs=[vmem_spec] * 2,
+        out_specs=[any_spec] * 2,
+        scratch_shapes=[pltpu.SemaphoreType.DMA((2,))],
+        name="finish",
+    )(*[pltpu.with_memory_space_constraint(o, pltpu.VMEM) for o in outs])
     return outs[0].reshape(width), outs[1].reshape(width)
 
 

time: 37.1 us -> 34.4 us (0.927)
  local copies, waits for them, and re-layouts: 2.65 us -> 0 us
    unnamed x2 -> x0, local copies, waits for them, and re-layouts: 2.65 us -> none
    pallas_call x0 -> x1, Pallas kernels: none -> 0.63 us  [shards(): pl.pallas_call(finish, out_shape=[jax.ShapeDtypeStruct((1, width), F32)]...]
    pallas_call x1, Pallas kernels: 33.5 us -> 32.9 us  [shards(): pl.pallas_call(functools.partial(kernel, (n_iface, n_dom, hist, base, row...]
where the time goes in v2:
time: 34.4 us; the launch traced here: 34.2 us
  Pallas kernels  33.6 us (98%)
  between operations  0.64 us (2%)
    pallas_call x1, Pallas kernels, shards(): pl.pallas_call(functools.partial(kernel, (n_iface, n_dom, hist, base, row...  32.9 us

profile of v2, /device:TPU:0, one launch (start us, length us, event | category | flops | bytes accessed | tf_op | source)
XLA Modules:
  0.0 34.2 jit_solution(3385137208443378453)
XLA Ops:
  0.6 32.9 %coupling.1 = (f32[1,4096]{1,0:T(1,128)S(1)}, f32[1,4096]{1,0:T(1,128)S(1)}) custom-call(f32[1,4096]{1,0:T(1,128)} %bitcast.7, f32[1,4096]{1,0:T(1,128)} %bitcast.8, f32[1,4096]{1,0:T(1,128)} %bitcast.9, f32[1,4096]{1,0:T(1,128)} %bitcast.10, f32[1,4096]{1,0:T(1,128)} %bitcast.11, f32[100,4096]{1,0:T(8,128)} %history_residual.1, f32[100,4096]{1,0:T(8,128)} %history_estimate.1), custom_call_target="tpu_custom_call" | custom-call | tf_op jit(solution)/shard_map/coupling/pallas_call | solution.py:361
  33.6 0.6 %finish.1 = (f32[1,4096]{1,0:T(1,128)}, f32[1,4096]{1,0:T(1,128)}) custom-call(f32[1,4096]{1,0:T(1,128)S(1)} %get-tuple-element.6.a, f32[1,4096]{1,0:T(1,128)S(1)} %get-tuple-element.7.b), custom_call_target="tpu_custom_call" | custom-call | tf_op jit(solution)/shard_map/finish/pallas_call | solution.py:403

commit v3 on v2

--- a/solution.py
+++ b/solution.py
@@ -126,14 +126,26 @@
     def add_gram(at, total):
         piece(at).wait()
         block = hist_v[:, pl.ds(pl.multiple_of(at * depth, depth), depth)]
-        return total + lax.dot_general(
-            block, block, (((1,), (1,)), ((), ())), precision=lax.Precision.HIGHEST, preferred_element_type=F32
+        one = block.astype(jnp.bfloat16)
+        rest = block - one.astype(F32)
+        two = rest.astype(jnp.bfloat16)
+        three = (rest - two.astype(F32)).astype(jnp.bfloat16)
+        main = jnp.concatenate([one, two], axis=1)
+        side = jnp.concatenate([two, three], axis=1), jnp.concatenate([one, one], axis=1)
+        dims = (((1,), (1,)), ((), ()))
+        return (
+            total[0] + lax.dot_general(main, main, dims, preferred_element_type=F32),
+            total[1] + lax.dot_general(*side, dims, preferred_element_type=F32),
         )
 
-    gram = lax.fori_loop(0, width // depth, add_gram, jnp.zeros((hist, hist), F32))
+    empty = jnp.zeros((hist, hist), F32)
+    main, side = lax.fori_loop(0, width // depth, add_gram, (empty, empty))
     load_w.start()
     square[...] = jnp.zeros(square.shape, F32)
-    square[0:hist, 0:hist] = gram
+    square[0:hist, 0:hist] = side
+    mirrored = square[...].T
+    square[0:hist, 0:hist] = main + side
+    square[...] = square[...] + mirrored
     lane8 = lax.broadcasted_iota(jnp.int32, (8, LANES), 1)
     blocks = (base // 8 + 1) // 2 * 2
     pairs = blocks // 2
@@ -273,11 +285,11 @@
     cur_x[...] = jnp.where(outside, 0.0, cur_x[...])
     begin(0)
     load_w.wait()
-    edges_start(wide)
     arrive(mid_in, n_iface - 1, mid_sem)
     gathered[at_dom] = jnp.sum(mid_in[...], axis=0)
     for dom in doms[1:]:
         send(gathered.at[at_dom], gathered.at[at_dom], gather_sem, (at_iface, dom))
+    edges_start(wide)
     arrive(gathered, n_dom - 1, gather_sem)
     for pair in range(pairs):
         other = blocks - 1 - pair
@@ -328,16 +340,21 @@
             weights = jnp.where(row_at == base + a, answer[a], weights - solved[a] * answer[a])
 
         def combine(at, carry):
-            span = pl.ds(pl.multiple_of(at * LANES, LANES), LANES)
-            cur_x[:, span] = (
-                est_x[:, span]
-                - over_rows(hist_w[:, span] * weights[0:hist, :])
-                - over_rows(new_w[:, span] * weights[base:rows, :])
-            )
+            span = pl.ds(at * LANES if isinstance(at, int) else pl.multiple_of(at * LANES, LANES), LANES)
+            total = new_w[:, span] * weights[base:rows, :]
+            for first in range(0, hist, 8):
+                some = min(8, hist - first)
+                term = hist_w[first : first + some, span] * weights[first : first + some, :]
+                if some < 8:
+                    term = jnp.concatenate([term, jnp.zeros((8 - some, LANES), F32)], axis=0)
+                total = total + term
+            cur_x[:, span] = est_x[:, span] - over_rows(total)
             return carry
 
-        lax.fori_loop(0, full // LANES, combine, 0, unroll=2)
+        lax.fori_loop(1, full // LANES - 1, combine, 0, unroll=4)
         if iteration + 1 < ITERS:
+            combine(0, 0)
+            combine(full // LANES - 1, 0)
             cur_x[...] = jnp.where(outside, 0.0, cur_x[...])
             begin(iteration + 1)
     next_ref[...] = cur_x[:, LANES : LANES + width]

time: 34.4 us -> 33.5 us (0.974)
  Pallas kernels: 33.6 us -> 32.7 us
    pallas_call x1, Pallas kernels: 32.9 us -> 32.1 us  [shards(): pl.pallas_call(functools.partial(kernel, (n_iface, n_dom, hist, base, row...]
where the time goes in v3:
time: 33.5 us; the launch traced here: 33.3 us
  Pallas kernels  32.7 us (98%)
  between operations  0.64 us (2%)
    pallas_call x1, Pallas kernels, shards(): pl.pallas_call(functools.partial(kernel, (n_iface, n_dom, hist, base, row...  32.1 us

profile of v3, /device:TPU:0, one launch (start us, length us, event | category | flops | bytes accessed | tf_op | source)
XLA Modules:
  0.0 33.3 jit_solution(4584705742418387286)
XLA Ops:
  0.6 32.1 %coupling.1 = (f32[1,4096]{1,0:T(1,128)S(1)}, f32[1,4096]{1,0:T(1,128)S(1)}) custom-call(f32[1,4096]{1,0:T(1,128)} %bitcast.7, f32[1,4096]{1,0:T(1,128)} %bitcast.8, f32[1,4096]{1,0:T(1,128)} %bitcast.9, f32[1,4096]{1,0:T(1,128)} %bitcast.10, f32[1,4096]{1,0:T(1,128)} %bitcast.11, f32[100,4096]{1,0:T(8,128)} %history_residual.1, f32[100,4096]{1,0:T(8,128)} %history_estimate.1), custom_call_target="tpu_custom_call" | custom-call | tf_op jit(solution)/shard_map/coupling/pallas_call | solution.py:378
  32.7 0.6 %finish.1 = (f32[1,4096]{1,0:T(1,128)}, f32[1,4096]{1,0:T(1,128)}) custom-call(f32[1,4096]{1,0:T(1,128)S(1)} %get-tuple-element.6.a, f32[1,4096]{1,0:T(1,128)S(1)} %get-tuple-element.7.b), custom_call_target="tpu_custom_call" | custom-call | tf_op jit(solution)/shard_map/finish/pallas_call | solution.py:420

commit v4 on v3

--- a/solution.py
+++ b/solution.py
@@ -95,8 +95,18 @@
         return (index // n_dom, lax.rem(index, n_dom))
 
     barrier = pltpu.get_barrier_semaphore()
-    for device in everyone:
+
+    def greet(device):
         pl.semaphore_signal(barrier, inc=1, device_id=device, device_id_type=pl.DeviceIdType.MESH)
+
+    for iface in ifaces[1:]:
+        greet((iface, at_dom))
+    right = place(lax.rem(me + 1, count))
+    left = place(lax.rem(me + last, count))
+    greet(right)
+    greet(left)
+    for dom in doms[1:]:
+        greet((at_iface, dom))
 
     own = pl.ds(LANES, width)
 
@@ -164,10 +174,7 @@
     part_in[at_dom] = part_out[at_dom]
     for copy in small:
         copy.wait()
-    pl.semaphore_wait(barrier, last)
-
-    right = place(lax.rem(me + 1, count))
-    left = place(lax.rem(me + last, count))
+    pl.semaphore_wait(barrier, n_iface + n_dom)
 
     def edges(refs, sems):
         copies = []

time: 33.5 us -> 33.4 us (level)
  no operation moved by 1% of the time
where the time goes in v4:
time: 33.4 us; the launch traced here: 33.3 us
  Pallas kernels  32.6 us (98%)
  between operations  0.64 us (2%)
    pallas_call x1, Pallas kernels, shards(): pl.pallas_call(functools.partial(kernel, (n_iface, n_dom, hist, base, row...  32 us

profile of v4, /device:TPU:0, one launch (start us, length us, event | category | flops | bytes accessed | tf_op | source)
XLA Modules:
  0.0 33.3 jit_solution(17774261696842907148)
XLA Ops:
  0.6 32.0 %coupling.1 = (f32[1,4096]{1,0:T(1,128)S(1)}, f32[1,4096]{1,0:T(1,128)S(1)}) custom-call(f32[1,4096]{1,0:T(1,128)} %bitcast.7, f32[1,4096]{1,0:T(1,128)} %bitcast.8, f32[1,4096]{1,0:T(1,128)} %bitcast.9, f32[1,4096]{1,0:T(1,128)} %bitcast.10, f32[1,4096]{1,0:T(1,128)} %bitcast.11, f32[100,4096]{1,0:T(8,128)} %history_residual.1, f32[100,4096]{1,0:T(8,128)} %history_estimate.1), custom_call_target="tpu_custom_call" | custom-call | tf_op jit(solution)/shard_map/coupling/pallas_call | solution.py:385
  32.6 0.6 %finish.1 = (f32[1,4096]{1,0:T(1,128)}, f32[1,4096]{1,0:T(1,128)}) custom-call(f32[1,4096]{1,0:T(1,128)S(1)} %get-tuple-element.6.a, f32[1,4096]{1,0:T(1,128)S(1)} %get-tuple-element.7.b), custom_call_target="tpu_custom_call" | custom-call | tf_op jit(solution)/shard_map/finish/pallas_call | solution.py:427
